TPU v7x, 32 devices: a whole 2x2x4 slice. The times are simulated.
32 devices in a mesh: tm: 8 (over z, x), space: 4 (over y, core).
Axes of the slice: x: 2, y: 2, z: 4, core: 2. Of those that a mesh axis runs over, the one named last changes fastest.
Arguments:
- state: float32 [32, 16, 64, 128], P('tm', 'space'), may hold values from -6 to 6
- source: float32 [32, 16, 64, 128], P('tm', 'space'), may hold values from -6 to 6
- absorption: float32 [16, 64, 128], P('space'), may hold values from 0.05 to 0.5
Outputs:
- relaxed: float32 [32, 16, 64, 128], P('tm', 'space')
- coarse_residual: float32 [8, 16, 64, 128], P('tm', 'space')
- residual_norm: float32 [], replicated
All inputs are finite; a program needn't handle non-finite values.
Results may differ from a plain program's by a relative error of at most 0.0004.
Values sent between devices are 32-bit elements; how exact they have to be, the bound alone decides.
A program may use at most 64 MiB of HBM per device.

v0:
```python
import math
import jax
import jax.numpy as jnp
from jax import lax
from jax.sharding import PartitionSpec as P

CF = 4
SWEEPS = 5
coupling = 4.0


def shifted(value, axis, by):
    count = lax.axis_size(axis)
    pairs = [(i, i + by) for i in range(count) if 0 <= i + by < count]
    return lax.ppermute(value, axis, pairs)


def sweep_weights(count):
    spread = 6.0 * coupling / (1.0 + 6.0 * coupling)
    return [
        1.0 / (1.0 + spread * math.cos(math.pi * (2 * k + 1) / (2 * count))) for k in range(count)
    ]


def apply_inner(extended, diag):
    inner = extended[1:-1]
    sides = jnp.pad(inner, ((0, 0), (1, 1), (1, 1)))
    beside = extended[2:] + extended[:-2]
    beside = beside + sides[:, 2:, 1:-1] + sides[:, :-2, 1:-1]
    beside = beside + sides[:, 1:-1, 2:] + sides[:, 1:-1, :-2]
    return diag * inner - coupling * beside


def step_whole(rhs, diag_full):
    field = rhs / diag_full
    for weight in sweep_weights(SWEEPS):
        extended = jnp.pad(field, ((1, 1), (0, 0), (0, 0)))
        field = field + weight * (rhs - apply_inner(extended, diag_full)) / diag_full
    return field


def local(state, source, absorption):
    depth_cells = absorption.shape[0]
    offset = lax.axis_index("space") * depth_cells

    def previous(last):
        return shifted(last, "tm", 1)

    stacked = jnp.concatenate([state[:1], source, absorption[None]], axis=0)
    gathered = lax.all_gather(stacked, "space", axis=1, tiled=True)
    source_full = gathered[1 : CF + 1]
    diag_full = 1.0 + 6.0 * coupling + gathered[CF + 1]

    def own_layers(field):
        return lax.dynamic_slice_in_dim(field, offset, depth_cells, 0)

    def back_full(last):
        return lax.all_gather(previous(own_layers(last)), "space", axis=0, tiled=True)

    points = [gathered[0]] + [None] * (CF - 1)

    def relax_full(points):
        for j in range(1, CF):
            points[j] = step_whole(points[j - 1], diag_full) + source_full[j]
        return points

    points = relax_full(points)
    points[0] = step_whole(back_full(points[-1]), diag_full) + source_full[0]
    points = relax_full(points)
    coarse_full = source_full[0] + step_whole(back_full(points[-1]), diag_full) - points[0]
    coarse_residual = own_layers(coarse_full)
    points = [own_layers(point) for point in points]
    residual_norm = lax.psum(jnp.sum(coarse_residual * coarse_residual), ("tm", "space"))
    relaxed = jnp.stack(points, axis=0)
    return (relaxed, coarse_residual[None], residual_norm)


def solution(mesh):
    return jax.shard_map(
        local,
        mesh=mesh,
        in_specs=(
            P("tm", "space", None, None),
            P("tm", "space", None, None),
            P("space", None, None),
        ),
        out_specs=(P("tm", "space", None, None), P("tm", "space", None, None), P()),
        check_vma=False,
    )
```

profile of v0, /device:TPU:0, one launch (start us, length us, event | category | flops | bytes accessed | tf_op | source)
XLA Modules:
  0.0 141.3 jit_solution(12284245266139244024)
XLA Ops:
  7.2 0.9 slice.790
  8.1 2.1 %pad_maximum_fusion = f32[6,4,64,128]{3,2,1,0:T(8,128)} fusion(f32[1,4,64,128]{3,2,1,0:T(8,128)} %bitcast.153, f32[4,4,64,128]{3,2,1,0:T(8,128)} %param.4, f32[1,4,64,128]{3,2,1,0:T(8,128)S(1)} %slice.790), kind=kLoop, calls=%fused_computation.160 | loop fusion | flops 393216 | bytes 1572864 | tf_op jit(solution)/shard_map/concatenate | solution.py:49
  10.2 31.4 %all-gather.2.cloned.1.call-done = f32[6,16,64,128]{3,2,1,0:T(8,128)} async-done(((f32[6,4,64,128]{3,2,1,0:T(8,128)}), f32[6,16,64,128]{3,2,1,0:T(8,128)}) %all-gather.2.cloned.1.call-update) | async-done | bytes 3145744 | tf_op jit(solution)/shard_map/all_gather | solution.py:50
  41.6 1.4 %fusion.424 = f32[16,64,128]{2,1,0:T(8,128)S(1)} fusion(f32[6,16,64,128]{3,2,1,0:T(8,128)} %all-gather.2.cloned.1.call-done), kind=kLoop, calls=%fused_computation.672 | loop fusion | flops 262144 | bytes 1572864 | tf_op jit(solution)/shard_map/div | solution.py:35
  43.1 1.6 %fusion.10 = f32[16,64,128]{2,1,0:T(8,128)S(1)} fusion(f32[16,64,128]{2,1,0:T(8,128)S(1)} %fusion.424, f32[6,16,64,128]{3,2,1,0:T(8,128)} %all-gather.2.cloned.1.call-done), kind=kLoop, calls=%fused_computation.251 | loop fusion | flops 1703936 | bytes 2097152 | tf_op jit(solution)/shard_map/add | solution.py:38
  44.7 0.4 fusion.21
  45.2 0.4 fusion.31
  46.0 0.4 fusion.443
  47.3 0.4 fusion.86
  48.2 0.4 fusion.441
  49.5 0.4 fusion.141
  50.0 0.5 fusion.439
  51.1 3.4 %collective-permute-start = (f32[4,64,128]{2,1,0:T(8,128)S(1)}, f32[4,64,128]{2,1,0:T(8,128)S(1)}, u32[]{:S(2)}, u32[]{:S(2)}) collective-permute-start(f32[4,64,128]{2,1,0:T(8,128)S(1)} %fusion.432), channel_id=1, source_target_pairs={{0,4},{4,8},{8,12},{12,16},{16,20},{20,24},{24,28},{1,5},{5,9},{9,... | collective-permute-start | bytes 393224 | tf_op jit(solution)/shard_map/ppermute | solution.py:15
  54.5 3.1 %collective-permute-done = f32[4,64,128]{2,1,0:T(8,128)S(1)} collective-permute-done((f32[4,64,128]{2,1,0:T(8,128)S(1)}, f32[4,64,128]{2,1,0:T(8,128)S(1)}, u32[]{:S(2)}, u32[]{:S(2)}) %collective-permute-start) | collective-permute-done | bytes 131104 | tf_op jit(solution)/shard_map/ppermute | solution.py:15
  57.6 6.7 %all_gather.10 = f32[16,64,128]{2,1,0:T(8,128)S(1)} all-gather(f32[4,64,128]{2,1,0:T(8,128)S(1)} %collective-permute-done), channel_id=1, replica_groups=mesh['tm'=8,'space'=4] {'space'}, dimensions={0}, use_global_device_ids=true | all-gather | bytes 655360 | tf_op jit(solution)/shard_map/all_gather | solution.py:58
  64.4 0.4 fusion.169
  64.8 0.4 fusion.180
  65.2 0.4 fusion.190
  66.1 0.4 fusion.435
  67.4 0.4 fusion.245
  68.3 0.4 fusion.442
  69.6 0.4 fusion.300
  70.5 0.4 fusion.436
  71.8 0.4 fusion.355
  72.3 0.5 fusion.440
  73.2 4.4 %collective-permute-start.1 = (f32[4,64,128]{2,1,0:T(8,128)S(1)}, f32[4,64,128]{2,1,0:T(8,128)S(1)}, u32[]{:S(2)}, u32[]{:S(2)}) collective-permute-start(f32[4,64,128]{2,1,0:T(8,128)S(1)} %get-tuple-element.24), channel_id=1, source_target_pairs={{0,4},{4,8},{8,12},{12,16},{16,20},{20,24},{24,28},{1,5},{5,9},{9,... | collective-permute-start | bytes 393224 | tf_op jit(solution)/shard_map/ppermute | solution.py:15
  77.6 3.2 %collective-permute-done.1 = f32[4,64,128]{2,1,0:T(8,128)S(1)} collective-permute-done((f32[4,64,128]{2,1,0:T(8,128)S(1)}, f32[4,64,128]{2,1,0:T(8,128)S(1)}, u32[]{:S(2)}, u32[]{:S(2)}) %collective-permute-start.1) | collective-permute-done | bytes 131104 | tf_op jit(solution)/shard_map/ppermute | solution.py:15
  80.8 6.9 %all_gather.11 = f32[16,64,128]{2,1,0:T(8,128)S(1)} all-gather(f32[4,64,128]{2,1,0:T(8,128)S(1)} %collective-permute-done.1), channel_id=1, replica_groups=mesh['tm'=8,'space'=4] {'space'}, dimensions={0}, use_global_device_ids=true | all-gather | bytes 655360 | tf_op jit(solution)/shard_map/all_gather | solution.py:58
  88.7 0.5 fusion.404
  90.0 1.3 multiply_reduce_fusion
  91.3 42.3 %psum.7 = f32[]{:T(128)} all-reduce(f32[]{:T(128)} %get-tuple-element.3), channel_id=1, replica_groups=mesh['tm'=8,'space'=4] {'tm','space'}, use_global_device_ids=true, to_apply=%region_1.2 | all-reduce | flops 1 | bytes 8 | tf_op jit(solution)/shard_map/psum | solution.py:73
  133.6 0.8 pad_maximum_fusion.1
  (31 shorter events, 9.3 us)
Async XLA Ops:
  7.2 34.5 %all-gather.2.cloned.1.call-start = ((), (), s32[]{:S(2)}) async-start(), calls=%async_computation | async-start | bytes 3932160 | tf_op jit(solution)/shard_map/all_gather | solution.py:50
  41.6 3.1 %copy-start = (f32[6,16,64,128]{3,2,1,0:T(8,128)S(1)}, f32[6,16,64,128]{3,2,1,0:T(8,128)}, u32[]{:S(2)}) copy-start(f32[6,16,64,128]{3,2,1,0:T(8,128)} %all-gather.2.cloned.1.call-done) | copy-start | bytes 9437188
  51.1 6.5 %collective-permute-start = (f32[4,64,128]{2,1,0:T(8,128)S(1)}, f32[4,64,128]{2,1,0:T(8,128)S(1)}, u32[]{:S(2)}, u32[]{:S(2)}) collective-permute-start(f32[4,64,128]{2,1,0:T(8,128)S(1)} %fusion.432), channel_id=1, source_target_pairs={{0,4},{4,8},{8,12},{12,16},{16,20},{20,24},{24,28},{1,5},{5,9},{9,... | collective-permute-start | bytes 393224 | tf_op jit(solution)/shard_map/ppermute | solution.py:15
  73.2 7.6 %collective-permute-start.1 = (f32[4,64,128]{2,1,0:T(8,128)S(1)}, f32[4,64,128]{2,1,0:T(8,128)S(1)}, u32[]{:S(2)}, u32[]{:S(2)}) collective-permute-start(f32[4,64,128]{2,1,0:T(8,128)S(1)} %get-tuple-element.24), channel_id=1, source_target_pairs={{0,4},{4,8},{8,12},{12,16},{16,20},{20,24},{24,28},{1,5},{5,9},{9,... | collective-permute-start | bytes 393224 | tf_op jit(solution)/shard_map/ppermute | solution.py:15
Sparse Core Ops, SparseCore 0:
  10.4 31.2 all-gather.1
where the time goes:
time: 142 us; the launch traced here: 141 us
  blocking collectives  55.8 us (39%)
  waiting for transfers between devices  37.7 us (27%)
  other arithmetic  24.6 us (17%)
  between operations  14.3 us (10%)
  starting transfers between devices  7.81 us (6%)
    psum x1, blocking collectives, local(): lax.psum(jnp.sum(coarse_residual * coarse_residual), ('tm', 'space'))  42.3 us
    all_gather x1, waiting for transfers between devices, local(): gathered = lax.all_gather(stacked, 'space', axis=1, tiled=True)  31.4 us
    add x30, other arithmetic, step_whole(): field + weight * (rhs - apply_inner(extended, diag_full)) / diag_full  14.2 us
    all_gather x2, blocking collectives, back_full(): lax.all_gather(previous(own_layers(last)), 'space', axis=0, tiled=True)  13.5 us
    ppermute x2, starting transfers between devices, shifted(): return lax.ppermute(value, axis, pairs)  7.77 us
    ppermute x2, waiting for transfers between devices, shifted(): return lax.ppermute(value, axis, pairs)  6.35 us
    div x8, other arithmetic, step_whole(): field = rhs / diag_full  3.89 us
  transfers between devices with their start and end apart: 3, of which 3 were waited for; matrix products, arithmetic and copies ran while one was open for 0% of the time, Pallas kernels for 0%

commit v1 on v0

--- a/solution.py
+++ b/solution.py
@@ -47,7 +47,14 @@
         return shifted(last, "tm", 1)
 
     stacked = jnp.concatenate([state[:1], source, absorption[None]], axis=0)
-    gathered = lax.all_gather(stacked, "space", axis=1, tiled=True)
+    ring = [stacked]
+    for hop in range(3):
+        ring.append(lax.ppermute(ring[-1], "space", [(dev, (dev + 1) % 4) for dev in range(4)]))
+    gathered = jnp.roll(
+        jnp.concatenate(ring[::-1], axis=1),
+        (lax.axis_index("space") + 1) * ring[0].shape[1],
+        axis=1,
+    )
     source_full = gathered[1 : CF + 1]
     diag_full = 1.0 + 6.0 * coupling + gathered[CF + 1]
 

time: 142 us -> 134 us (0.944)
  between operations: 14.3 us -> 1.1 us
  waiting for transfers between devices: 37.7 us -> 40.2 us
    ppermute x0 -> x3, waiting for transfers between devices: none -> 34.4 us  [local(): lax.ppermute(ring[-1], 'space', [(dev, (dev + 1) % 4) for dev in range(4)])]
    all_gather x1 -> x0, waiting for transfers between devices: 31.4 us -> none  [local(): gathered = lax.all_gather(stacked, 'space', axis=1, tiled=True)]
    div x8, other arithmetic: 3.89 us -> 5.79 us  [step_whole(): field = rhs / diag_full]
  transfers between devices with their start and end apart: 3 -> 5, of which waited for: 3 -> 5; matrix products, arithmetic and copies ran while one was open for 0% -> 0% of each run, Pallas kernels for 0% -> 0%
where the time goes in v1:
time: 134 us
  blocking collectives  56.3 us (42%)
  waiting for transfers between devices  40.2 us (30%)
  other arithmetic  24.6 us (18%)
  starting transfers between devices  9.09 us (7%)
  local copies, waits for them, and re-layouts  2.32 us (2%)
    psum x1, blocking collectives, local(): lax.psum(jnp.sum(coarse_residual * coarse_residual), ('tm', 'space'))  42.5 us
    ppermute x3, waiting for transfers between devices, local(): lax.ppermute(ring[-1], 'space', [(dev, (dev + 1) % 4) for dev in range(4)])  34.4 us
    all_gather x2, blocking collectives, back_full(): lax.all_gather(previous(own_layers(last)), 'space', axis=0, tiled=True)  13.9 us
    add x30, other arithmetic, step_whole(): field + weight * (rhs - apply_inner(extended, diag_full)) / diag_full  13.3 us
    ppermute x2, starting transfers between devices, shifted(): return lax.ppermute(value, axis, pairs)  8.54 us
    div x8, other arithmetic, step_whole(): field = rhs / diag_full  5.79 us
    ppermute x2, waiting for transfers between devices, shifted(): return lax.ppermute(value, axis, pairs)  5.71 us
  transfers between devices with their start and end apart: 5, of which 5 were waited for; matrix products, arithmetic and copies ran while one was open for 0% of the time, Pallas kernels for 0%

profile of v1, /device:TPU:0, one launch (start us, length us, event | category | flops | bytes accessed | tf_op | source)
XLA Modules:
  0.0 133.6 jit_solution(3934758007386616674)
XLA Ops:
  0.6 0.9 slice.790
  1.5 1.2 pad_maximum_fusion
  2.7 0.5 collective-permute-start
  3.3 11.6 %collective-permute-done = f32[6,4,64,128]{3,2,1,0:T(8,128)S(1)} collective-permute-done((f32[6,4,64,128]{3,2,1,0:T(8,128)S(1)}, f32[6,4,64,128]{3,2,1,0:T(8,128)S(1)}, u32[]{:S(2)}, u32[]{:S(2)}) %collective-permute-start) | collective-permute-done | bytes 786464 | tf_op jit(solution)/shard_map/ppermute | solution.py:52
  14.9 11.4 %collective-permute-done.1 = f32[6,4,64,128]{3,2,1,0:T(8,128)S(1)} collective-permute-done((f32[6,4,64,128]{3,2,1,0:T(8,128)S(1)}, f32[6,4,64,128]{3,2,1,0:T(8,128)S(1)}, u32[]{:S(2)}, u32[]{:S(2)}) %collective-permute-start.1) | collective-permute-done | bytes 786464 | tf_op jit(solution)/shard_map/ppermute | solution.py:52
  26.3 11.4 %collective-permute-done.2 = f32[6,4,64,128]{3,2,1,0:T(8,128)S(1)} collective-permute-done((f32[6,4,64,128]{3,2,1,0:T(8,128)S(1)}, f32[6,4,64,128]{3,2,1,0:T(8,128)S(1)}, u32[]{:S(2)}, u32[]{:S(2)}) %collective-permute-start.2) | collective-permute-done | bytes 786464 | tf_op jit(solution)/shard_map/ppermute | solution.py:52
  38.0 0.8 copy-done.1
  39.4 0.5 fusion.10
  39.9 0.5 fusion.21
  40.3 0.5 fusion.31
  40.8 0.5 fusion.42
  41.2 0.5 fusion.448
  42.6 0.5 fusion.86
  43.5 0.5 fusion.446
  44.8 0.5 fusion.141
  45.3 0.5 fusion.444
  46.2 4.2 %collective-permute-start.3 = (f32[4,64,128]{2,1,0:T(8,128)S(1)}, f32[4,64,128]{2,1,0:T(8,128)S(1)}, u32[]{:S(2)}, u32[]{:S(2)}) collective-permute-start(f32[4,64,128]{2,1,0:T(8,128)S(1)} %fusion.432), channel_id=1, source_target_pairs={{0,4},{4,8},{8,12},{12,16},{16,20},{20,24},{24,28},{1,5},{5,9},{9,... | collective-permute-start | bytes 393224 | tf_op jit(solution)/shard_map/ppermute | solution.py:15
  50.4 2.5 %collective-permute-done.3 = f32[4,64,128]{2,1,0:T(8,128)S(1)} collective-permute-done((f32[4,64,128]{2,1,0:T(8,128)S(1)}, f32[4,64,128]{2,1,0:T(8,128)S(1)}, u32[]{:S(2)}, u32[]{:S(2)}) %collective-permute-start.3) | collective-permute-done | bytes 131104 | tf_op jit(solution)/shard_map/ppermute | solution.py:15
  52.9 7.4 %all_gather.6 = f32[16,64,128]{2,1,0:T(8,128)S(1)} all-gather(f32[4,64,128]{2,1,0:T(8,128)S(1)} %collective-permute-done.3), channel_id=1, replica_groups=mesh['tm'=8,'space'=4] {'space'}, dimensions={0}, use_global_device_ids=true | all-gather | bytes 655360 | tf_op jit(solution)/shard_map/all_gather | solution.py:65
  61.3 0.5 fusion.190
  62.2 1.5 %fusion.442 = (f32[16,64,128]{2,1,0:T(8,128)S(1)}, f32[16,64,128]{2,1,0:T(8,128)S(1)}, f32[16,64,128]{2,1,0:T(8,128)S(1)}) fusion(f32[16,64,128]{2,1,0:T(8,128)S(1)} %get-tuple-element.21, f32[16,64,128]{2,1,0:T(8,128)S(1)} %fusion.201, f32[16,64,128]{2,1,0:T(8,128)S(1)} %all_gather.6, f32[6,32,64,128]{3,2,1,0:T(8,128)} %copy-done, s32[]{:T(128)S(6)} %add.1196, ...), kind=kLoop, calls=%fused_computation.706 | loop fusion | flops 1835008 | bytes 3670024 | tf_op jit(solution)/shard_map/div | solution.py:35
  64.7 0.5 fusion.245
  65.6 1.5 %fusion.440 = (f32[16,64,128]{2,1,0:T(8,128)S(1)}, f32[16,64,128]{2,1,0:T(8,128)S(1)}) fusion(f32[16,64,128]{2,1,0:T(8,128)S(1)} %get-tuple-element.21, f32[6,32,64,128]{3,2,1,0:T(8,128)} %copy-done, s32[]{:T(128)S(6)} %add.1193, s32[]{:T(128)S(6)} %select_n.23, f32[16,64,128]{2,1,0:T(8,128)S(1)} %fusion.256, f32[16,64,128]{2,1,0:T(8,128)S(1)} %get-tuple-element.12), kind=kLoop, calls=%fused_computation.705 | loop fusion | flops 1835008 | bytes 3145736 | tf_op jit(solution)/shard_map/div | solution.py:35
  68.0 0.5 fusion.300
  68.9 1.5 %fusion.438 = (f32[16,64,128]{2,1,0:T(8,128)S(1)}, f32[16,64,128]{2,1,0:T(8,128)S(1)}) fusion(f32[16,64,128]{2,1,0:T(8,128)S(1)} %get-tuple-element.21, f32[6,32,64,128]{3,2,1,0:T(8,128)} %copy-done, s32[]{:T(128)S(6)} %add.1194, s32[]{:T(128)S(6)} %select_n.23, f32[16,64,128]{2,1,0:T(8,128)S(1)} %fusion.311, f32[16,64,128]{2,1,0:T(8,128)S(1)} %get-tuple-element.10), kind=kLoop, calls=%fused_computation.704 | loop fusion | flops 1835008 | bytes 3145736 | tf_op jit(solution)/shard_map/div | solution.py:35
  71.3 0.5 fusion.355
  72.6 4.4 %collective-permute-start.4 = (f32[4,64,128]{2,1,0:T(8,128)S(1)}, f32[4,64,128]{2,1,0:T(8,128)S(1)}, u32[]{:S(2)}, u32[]{:S(2)}) collective-permute-start(f32[4,64,128]{2,1,0:T(8,128)S(1)} %get-tuple-element.24), channel_id=1, source_target_pairs={{0,4},{4,8},{8,12},{12,16},{16,20},{20,24},{24,28},{1,5},{5,9},{9,... | collective-permute-start | bytes 393224 | tf_op jit(solution)/shard_map/ppermute | solution.py:15
  77.0 3.2 %collective-permute-done.4 = f32[4,64,128]{2,1,0:T(8,128)S(1)} collective-permute-done((f32[4,64,128]{2,1,0:T(8,128)S(1)}, f32[4,64,128]{2,1,0:T(8,128)S(1)}, u32[]{:S(2)}, u32[]{:S(2)}) %collective-permute-start.4) | collective-permute-done | bytes 131104 | tf_op jit(solution)/shard_map/ppermute | solution.py:15
  80.2 6.5 %all_gather.7 = f32[16,64,128]{2,1,0:T(8,128)S(1)} all-gather(f32[4,64,128]{2,1,0:T(8,128)S(1)} %collective-permute-done.4), channel_id=1, replica_groups=mesh['tm'=8,'space'=4] {'space'}, dimensions={0}, use_global_device_ids=true | all-gather | bytes 655360 | tf_op jit(solution)/shard_map/all_gather | solution.py:65
  89.0 1.3 multiply_reduce_fusion
  90.3 42.5 %psum.7 = f32[]{:T(128)} all-reduce(f32[]{:T(128)} %get-tuple-element.3), channel_id=1, replica_groups=mesh['tm'=8,'space'=4] {'tm','space'}, use_global_device_ids=true, to_apply=%region_1.2 | all-reduce | flops 1 | bytes 8 | tf_op jit(solution)/shard_map/psum | solution.py:80
  132.8 0.8 pad_maximum_fusion.1
  (46 shorter events, 11.4 us)
Async XLA Ops:
  2.7 12.2 %collective-permute-start = (f32[6,4,64,128]{3,2,1,0:T(8,128)S(1)}, f32[6,4,64,128]{3,2,1,0:T(8,128)S(1)}, u32[]{:S(2)}, u32[]{:S(2)}) collective-permute-start(f32[6,4,64,128]{3,2,1,0:T(8,128)S(1)} %pad_maximum_fusion), channel_id=1, source_target_pairs={{0,1},{1,2},{2,3},{3,0},{4,5},{5,6},{6,7},{7,4},{8,9},{9,10},{10,1... | collective-permute-start | bytes 2359304 | tf_op jit(solution)/shard_map/ppermute | solution.py:52
  14.9 11.4 %collective-permute-start.1 = (f32[6,4,64,128]{3,2,1,0:T(8,128)S(1)}, f32[6,4,64,128]{3,2,1,0:T(8,128)S(1)}, u32[]{:S(2)}, u32[]{:S(2)}) collective-permute-start(f32[6,4,64,128]{3,2,1,0:T(8,128)S(1)} %collective-permute-done), channel_id=1, source_target_pairs={{0,1},{1,2},{2,3},{3,0},{4,5},{5,6},{6,7},{7,4},{8,9},{9,10},{10,1... | collective-permute-start | bytes 2359304 | tf_op jit(solution)/shard_map/ppermute | solution.py:52
  26.3 11.4 %collective-permute-start.2 = (f32[6,4,64,128]{3,2,1,0:T(8,128)S(1)}, f32[6,4,64,128]{3,2,1,0:T(8,128)S(1)}, u32[]{:S(2)}, u32[]{:S(2)}) collective-permute-start(f32[6,4,64,128]{3,2,1,0:T(8,128)S(1)} %collective-permute-done.1), channel_id=1, source_target_pairs={{0,1},{1,2},{2,3},{3,0},{4,5},{5,6},{6,7},{7,4},{8,9},{9,10},{10,1... | collective-permute-start | bytes 2359304 | tf_op jit(solution)/shard_map/ppermute | solution.py:52
  37.8 1.0 copy-start.1
  37.8 1.1 copy-start.2
  39.2 6.9 %copy-start = (f32[6,32,64,128]{3,2,1,0:T(8,128)}, f32[6,32,64,128]{3,2,1,0:T(8,128)S(1)}, u32[]{:S(2)}) copy-start(f32[6,32,64,128]{3,2,1,0:T(8,128)S(1)} %constant_dynamic-update-slice_fusion) | copy-start | bytes 18874372
  46.2 6.7 %collective-permute-start.3 = (f32[4,64,128]{2,1,0:T(8,128)S(1)}, f32[4,64,128]{2,1,0:T(8,128)S(1)}, u32[]{:S(2)}, u32[]{:S(2)}) collective-permute-start(f32[4,64,128]{2,1,0:T(8,128)S(1)} %fusion.432), channel_id=1, source_target_pairs={{0,4},{4,8},{8,12},{12,16},{16,20},{20,24},{24,28},{1,5},{5,9},{9,... | collective-permute-start | bytes 393224 | tf_op jit(solution)/shard_map/ppermute | solution.py:15
  72.6 7.6 %collective-permute-start.4 = (f32[4,64,128]{2,1,0:T(8,128)S(1)}, f32[4,64,128]{2,1,0:T(8,128)S(1)}, u32[]{:S(2)}, u32[]{:S(2)}) collective-permute-start(f32[4,64,128]{2,1,0:T(8,128)S(1)} %get-tuple-element.24), channel_id=1, source_target_pairs={{0,4},{4,8},{8,12},{12,16},{16,20},{20,24},{24,28},{1,5},{5,9},{9,... | collective-permute-start | bytes 393224 | tf_op jit(solution)/shard_map/ppermute | solution.py:15
